TPU v7x, 512 devices: a 4x2x32 block of a 4x8x32 slice. The times are simulated.
512 devices in a mesh: groups: 2 (over y), batch: 128 (over z, x), mp: 2 (over core).
Axes of the slice: x: 4, y: 2, z: 32, core: 2. Of those that a mesh axis runs over, the one named last changes fastest.
The devices are a block of a 4x8x32 slice.
Arguments:
- hidden: bfloat16 [512, 1280], P(('groups', 'batch')), parts along dimension 0, may hold values from -6 to 6
- token_qkv: bfloat16 [3, 512, 1280], P(None, ('groups', 'batch'), 'mp'), parts along dimension 1, may hold values from -6 to 6
- self_cache: bfloat16 [2, 512, 128, 1280], P(None, ('groups', 'batch'), None, 'mp'), parts along dimension 1, may hold values from -6 to 6
- cross_kv: bfloat16 [2, 512, 64, 1280], P(None, ('groups', 'batch'), None, 'mp'), parts along dimension 1, may hold values from -6 to 6
- cache_len: int32 [512], P(('groups', 'batch')), parts along dimension 0, may hold values from 1 to 127
- finished: int32 [512], P(('groups', 'batch')), parts along dimension 0, may hold values 0 or 1
- new_slot: int32 [512], P(('groups', 'batch')), parts along dimension 0, may hold values from 0 to 255, as said below
- out_proj: bfloat16 [1280, 1280], P('mp'), may hold values from -0.15625 to 0.15625
- ln_gain: float32 [1280], replicated, may hold values from 0.5 to 1.5
- ln_bias: float32 [1280], replicated, may hold values from -3 to 3
- query_proj: bfloat16 [1280, 1280], P(None, 'mp'), may hold values from -3 to 3
Outputs:
- moved_cache: bfloat16 [2, 512, 128, 1280], P(None, ('groups', 'batch'), None, 'mp'), parts along dimension 1
- moved_out: bfloat16 [512, 1280], P(('groups', 'batch'), 'mp'), parts along dimension 0
There are 2 independent parts, one for each index of `groups`. A program takes and returns all parts, laid end to end along the dimension named above; an argument that names none is the same for every part. Nothing has to cross between parts.
Inputs may be any that keep to these rules, and one draw needn't show every extreme that they name: A permutation of the spans' slots. Span c's new owner new_slot[c] // 2 lies within 3 devices of its present one c // 2, counting the device order as a loop; of one device's spans at most one moves by any given signed distance.
All inputs are finite; a program needn't handle non-finite values. No bound on the sum of `finished` on one device may be relied on, other than what follows from the above.
Results may differ from a plain program's by a relative error of at most 0.015.
Values may be sent and summed in bfloat16 or wider, within the bound.
A program may use at most 64 MiB of HBM per device.

v0:
```python
import jax
import jax.numpy as jnp
from jax import lax
from jax.sharding import PartitionSpec as P

HEAD_DIM = 64
REACH = 3


def copy_for_each(array, axis):
    copies = jnp.broadcast_to(array, (lax.axis_size(axis), *array.shape))
    return lax.all_to_all(copies, axis, split_axis=0, concat_axis=0, tiled=True)


def of_everyone(array, axis):
    return copy_for_each(array, axis).sum(axis=0)


def passed_along(block, axis, distance):
    devices = range(lax.axis_size(axis))
    route = [((i - distance) % len(devices), i) for i in devices]
    return lax.ppermute(block, axis, route)


def body(
    hidden,
    token_qkv,
    self_cache,
    cross_kv,
    cache_len,
    finished,
    new_slot,
    out_proj,
    ln_gain,
    ln_bias,
    query_proj,
):
    spans = hidden.shape[0]
    slots = self_cache.shape[2]
    local_width = self_cache.shape[3]
    frames = cross_kv.shape[2]
    head_count = local_width // HEAD_DIM
    factor = HEAD_DIM ** (-0.5)
    new_query = token_qkv[0].reshape(spans, head_count, HEAD_DIM)
    new_key = token_qkv[1].reshape(spans, head_count, HEAD_DIM)
    new_value = token_qkv[2].reshape(spans, head_count, HEAD_DIM)
    cache_keys = self_cache[0].reshape(spans, slots, head_count, HEAD_DIM)
    cache_values = self_cache[1].reshape(spans, slots, head_count, HEAD_DIM)
    scores = (
        jnp.einsum("chd,cthd->cht", new_query, cache_keys, preferred_element_type=jnp.float32)
        * factor
    )
    position = jnp.arange(slots, dtype=jnp.int32)
    usable = position[None, None, :] < cache_len[:, None, None]
    scores = jnp.where(usable, scores, -1e30)
    own_score = (
        jnp.sum(new_query.astype(jnp.float32) * new_key.astype(jnp.float32), axis=-1) * factor
    )
    highest = jnp.maximum(jnp.max(scores, axis=-1), own_score)
    cache_weight = jnp.where(usable, jnp.exp(scores - highest[..., None]), 0.0)
    own_weight = jnp.exp(own_score - highest)
    total = jnp.sum(cache_weight, axis=-1) + own_weight
    cache_weight = (cache_weight / total[..., None]).astype(jnp.bfloat16)
    own_weight = (own_weight / total).astype(jnp.bfloat16)
    context = jnp.einsum(
        "cht,cthd->chd", cache_weight, cache_values, preferred_element_type=jnp.float32
    )
    context = context + own_weight.astype(jnp.float32)[..., None] * new_value.astype(jnp.float32)
    context = context.astype(jnp.bfloat16).reshape(spans, local_width)
    partial_proj = jnp.dot(context, out_proj, preferred_element_type=jnp.float32)
    resid = hidden.astype(jnp.float32) + of_everyone(partial_proj, "mp")
    centre = jnp.mean(resid, axis=-1, keepdims=True)
    spread = jnp.mean((resid - centre) ** 2, axis=-1, keepdims=True)
    normed = ((resid - centre) * lax.rsqrt(spread + 1e-05) * ln_gain + ln_bias).astype(jnp.bfloat16)
    cross_query = jnp.dot(normed, query_proj, preferred_element_type=jnp.float32).astype(
        jnp.bfloat16
    )
    cross_query = cross_query.reshape(spans, head_count, HEAD_DIM)
    cross_keys = cross_kv[0].reshape(spans, frames, head_count, HEAD_DIM)
    cross_values = cross_kv[1].reshape(spans, frames, head_count, HEAD_DIM)
    cross_scores = (
        jnp.einsum("chd,cthd->cht", cross_query, cross_keys, preferred_element_type=jnp.float32)
        * factor
    )
    cross_high = jnp.max(cross_scores, axis=-1, keepdims=True)
    cross_exp = jnp.exp(cross_scores - cross_high)
    cross_weight = (cross_exp / jnp.sum(cross_exp, axis=-1, keepdims=True)).astype(jnp.bfloat16)
    cross_context = jnp.einsum(
        "cht,cthd->chd", cross_weight, cross_values, preferred_element_type=jnp.float32
    )
    cross_context = cross_context.reshape(spans, local_width)
    alive = finished == 0
    decoded = jnp.where(alive[:, None], cross_context, 0.0).astype(jnp.bfloat16)
    slot_pos = position[None, :, None]
    length = cache_len[:, None, None]

    def extend(older, fresh):
        grown = jnp.where(
            slot_pos < length,
            older,
            jnp.where(slot_pos == length, fresh[:, None, :], jnp.zeros_like(older)),
        )
        return jnp.where(alive[:, None, None], grown, jnp.zeros_like(older))

    updated = jnp.stack([extend(self_cache[0], token_qkv[1]), extend(self_cache[1], token_qkv[2])])
    device_index = lax.axis_index("batch")
    device_count = lax.axis_size("batch")
    dest_device = new_slot // spans
    dest_local = new_slot % spans
    half_count = device_count // 2
    offset = (dest_device - device_index + half_count) % device_count - half_count
    placing = dest_local[:, None] == jnp.arange(spans, dtype=jnp.int32)[None, :]
    select = ((offset == 0)[:, None] & placing).astype(jnp.bfloat16)
    cache_part = jnp.einsum("jl,ajtd->altd", select, updated, preferred_element_type=jnp.float32)
    out_part = jnp.einsum("jl,jd->ld", select, decoded, preferred_element_type=jnp.float32)
    cache_total = cache_part
    out_total = out_part
    distances = [shift_by for shift_by in range(-REACH, REACH + 1) if shift_by != 0]
    placing_weights = placing.astype(jnp.bfloat16)
    for distance in distances:
        picked = (offset == distance).astype(jnp.bfloat16)
        payload = jnp.einsum(
            "j,ajtd->atd", picked, updated, preferred_element_type=jnp.float32
        ).astype(jnp.bfloat16)
        out_row = jnp.einsum("j,jd->d", picked, decoded, preferred_element_type=jnp.float32).astype(
            jnp.bfloat16
        )
        marker = jnp.einsum(
            "j,jl->l", picked, placing_weights, preferred_element_type=jnp.float32
        ).astype(jnp.bfloat16)
        marker_row = jnp.pad(marker, (0, local_width - spans))
        parcel = jnp.concatenate(
            [payload.reshape(2 * slots, local_width), out_row[None, :], marker_row[None, :]], 0
        )
        arrived = passed_along(parcel, "batch", distance)
        got_cache = arrived[: 2 * slots].reshape(2, slots, local_width)
        got_out = arrived[2 * slots]
        got_marker = arrived[2 * slots + 1, :spans]
        cache_total = cache_total + jnp.einsum(
            "l,atd->altd", got_marker, got_cache, preferred_element_type=jnp.float32
        )
        out_total = out_total + jnp.einsum(
            "l,d->ld", got_marker, got_out, preferred_element_type=jnp.float32
        )
    return (cache_total.astype(jnp.bfloat16), out_total.astype(jnp.bfloat16))


def solution(mesh):
    placed = (
        P(("groups", "batch"), None),
        P(None, ("groups", "batch"), "mp"),
        P(None, ("groups", "batch"), None, "mp"),
        P(None, ("groups", "batch"), None, "mp"),
        P(("groups", "batch")),
        P(("groups", "batch")),
        P(("groups", "batch")),
        P("mp", None),
        P(),
        P(),
        P(None, "mp"),
    )
    return jax.shard_map(
        body,
        mesh=mesh,
        in_specs=placed,
        out_specs=(P(None, ("groups", "batch"), None, "mp"), P(("groups", "batch"), "mp")),
        check_vma=False,
    )
```

profile of v0, /device:TPU:40, one launch (start us, length us, event | category | flops | bytes accessed | tf_op | source)
XLA Modules:
  0.0 108.2 jit_solution(13605991024664097077)
XLA Ops:
  0.6 0.8 slice_bitcast_fusion.1
  2.6 1.2 %fusion.108 = (bf16[1,2,128,640]{3,2,1,0:T(8,128)(2,1)S(1)}, bf16[1,2,128,640]{3,2,1,0:T(8,128)(2,1)S(1)}) fusion(bf16[2,2,128,640]{3,2,1,0:T(8,128)(2,1)} %param.13), kind=kLoop, calls=%fused_computation.188 | loop fusion | bytes 1310720 | tf_op jit(solution)/shard_map/slice | solution.py:105
  6.7 3.3 %all-to-all-start = ((f32[2,2,1280]{2,1,0:T(2,128)}), f32[2,2,1280]{2,1,0:T(2,128)S(1)}, u32[]{:S(2)}, u32[]{:S(2)}) async-start(f32[2,2,1280]{2,1,0:T(2,128)} %broadcast_in_dim.149), calls=%async_computation | async-start | bytes 40960 | tf_op jit(solution)/shard_map/all_to_all | solution.py:12
  11.7 1.8 %convolution_convert_fusion = bf16[2,640]{1,0:T(2,128)(2,1)S(1)} fusion(bf16[1280,640]{1,0:T(8,128)(2,1)} %param.21, f32[2]{0:T(128)S(1)} %add_rsqrt_fusion, f32[2]{0:T(128)S(1)} %broadcast_multiply_fusion, f32[1280]{0:T(1024)S(1)} %copy-done.3, f32[1280]{0:T(1024)S(1)} %copy-done.4, f32[2,1280]{1,0:T(2,128)S(1)} %reduce_sum.56, ...), kind=kOutput, calls=%fused_computation.8 | convolution fusion | flops 3296000 | bytes 1666576 | tf_op jit(solution)/shard_map/dot_general | solution.py:75
  14.6 1.4 %broadcast_select_fusion.5 = (bf16[1,2,128,640]{3,1,2,0:T(2,128)(2,1)S(1)}, bf16[1,2,128,640]{3,1,2,0:T(2,128)(2,1)S(1)}) fusion(pred[2]{0:T(512)(128)(4,1)S(1)} %broadcast_compare_fusion.7, pred[2,128]{0,1:T(8,128)(4,1)S(1)} %get-tuple-element.30, pred[2,128]{0,1:T(8,128)(4,1)S(1)} %get-tuple-element.29, bf16[1,2,128,640]{3,2,1,0:T(8,128)(2,1)S(1)} %get-tuple-element.16, ...), kind=kLoop, calls=%fused_computation.39 | loop fusion | flops 983040 | bytes 1316354 | tf_op jit(solution)/shard_map/jit(_where)/select_n | solution.py:103
  16.0 0.9 pad_maximum_fusion
  17.0 0.8 fusion.49
  17.9 5.1 %collective-permute-start.5 = (bf16[258,640]{1,0:T(8,128)(2,1)S(1)}, bf16[258,640]{1,0:T(8,128)(2,1)S(1)}, u32[]{:S(2)}, u32[]{:S(2)}) collective-permute-start(bf16[258,640]{1,0:T(8,128)(2,1)S(1)} %pad_maximum_fusion.6), channel_id=1, source_target_pairs={{250,0},{252,2},{254,4},{0,6},{2,8},{4,10},{6,12},{8,14},{10,16},{... | collective-permute-start | bytes 990728 | tf_op jit(solution)/shard_map/ppermute | solution.py:22
  23.3 0.8 fusion.51
  24.2 4.7 %collective-permute-start.4 = (bf16[258,640]{1,0:T(8,128)(2,1)S(1)}, bf16[258,640]{1,0:T(8,128)(2,1)S(1)}, u32[]{:S(2)}, u32[]{:S(2)}) collective-permute-start(bf16[258,640]{1,0:T(8,128)(2,1)S(1)} %pad_maximum_fusion.5), channel_id=1, source_target_pairs={{252,0},{254,2},{0,4},{2,6},{4,8},{6,10},{8,12},{10,14},{12,16},{1... | collective-permute-start | bytes 990728 | tf_op jit(solution)/shard_map/ppermute | solution.py:22
  29.2 0.8 fusion.53
  30.2 3.0 %collective-permute-start.3 = (bf16[258,640]{1,0:T(8,128)(2,1)S(1)}, bf16[258,640]{1,0:T(8,128)(2,1)S(1)}, u32[]{:S(2)}, u32[]{:S(2)}) collective-permute-start(bf16[258,640]{1,0:T(8,128)(2,1)S(1)} %pad_maximum_fusion.4), channel_id=1, source_target_pairs={{254,0},{0,2},{2,4},{4,6},{6,8},{8,10},{10,12},{12,14},{14,16},{16... | collective-permute-start | bytes 990728 | tf_op jit(solution)/shard_map/ppermute | solution.py:22
  33.4 0.8 fusion.55
  34.3 41.0 %collective-permute-start.2 = (bf16[258,640]{1,0:T(8,128)(2,1)S(1)}, bf16[258,640]{1,0:T(8,128)(2,1)S(1)}, u32[]{:S(2)}, u32[]{:S(2)}) collective-permute-start(bf16[258,640]{1,0:T(8,128)(2,1)S(1)} %pad_maximum_fusion.3), channel_id=1, source_target_pairs={{2,0},{4,2},{6,4},{8,6},{10,8},{12,10},{14,12},{16,14},{18,16},{20... | collective-permute-start | bytes 990728 | tf_op jit(solution)/shard_map/ppermute | solution.py:22
  75.7 0.8 fusion.57
  76.6 4.9 %collective-permute-start.1 = (bf16[258,640]{1,0:T(8,128)(2,1)S(1)}, bf16[258,640]{1,0:T(8,128)(2,1)S(1)}, u32[]{:S(2)}, u32[]{:S(2)}) collective-permute-start(bf16[258,640]{1,0:T(8,128)(2,1)S(1)} %pad_maximum_fusion.2), channel_id=1, source_target_pairs={{4,0},{6,2},{8,4},{10,6},{12,8},{14,10},{16,12},{18,14},{20,16},{2... | collective-permute-start | bytes 990728 | tf_op jit(solution)/shard_map/ppermute | solution.py:22
  81.8 0.8 fusion.59
  82.7 4.8 %collective-permute-start = (bf16[258,640]{1,0:T(8,128)(2,1)S(1)}, bf16[258,640]{1,0:T(8,128)(2,1)S(1)}, u32[]{:S(2)}, u32[]{:S(2)}) collective-permute-start(bf16[258,640]{1,0:T(8,128)(2,1)S(1)} %pad_maximum_fusion.1), channel_id=1, source_target_pairs={{6,0},{8,2},{10,4},{12,6},{14,8},{16,10},{18,12},{20,14},{22,16},{... | collective-permute-start | bytes 990728 | tf_op jit(solution)/shard_map/ppermute | solution.py:22
  87.8 5.2 %collective-permute-done.3 = bf16[258,640]{1,0:T(8,128)(2,1)S(1)} collective-permute-done((bf16[258,640]{1,0:T(8,128)(2,1)S(1)}, bf16[258,640]{1,0:T(8,128)(2,1)S(1)}, u32[]{:S(2)}, u32[]{:S(2)}) %collective-permute-start.3) | collective-permute-done | bytes 330272 | tf_op jit(solution)/shard_map/ppermute | solution.py:22
  93.2 2.8 %collective-permute-done.1 = bf16[258,640]{1,0:T(8,128)(2,1)S(1)} collective-permute-done((bf16[258,640]{1,0:T(8,128)(2,1)S(1)}, bf16[258,640]{1,0:T(8,128)(2,1)S(1)}, u32[]{:S(2)}, u32[]{:S(2)}) %collective-permute-start.1) | collective-permute-done | bytes 330272 | tf_op jit(solution)/shard_map/ppermute | solution.py:22
  96.1 7.1 %collective-permute-done = bf16[258,640]{1,0:T(8,128)(2,1)S(1)} collective-permute-done((bf16[258,640]{1,0:T(8,128)(2,1)S(1)}, bf16[258,640]{1,0:T(8,128)(2,1)S(1)}, u32[]{:S(2)}, u32[]{:S(2)}) %collective-permute-start) | collective-permute-done | bytes 330272 | tf_op jit(solution)/shard_map/ppermute | solution.py:22
  103.3 3.1 %fusion.13 = bf16[2,2,128,640]{3,1,2,0:T(2,128)(2,1)S(1)} fusion(f32[2]{0:T(128)S(1)} %fusion.70, f32[2,128,640]{2,1,0:T(8,128)S(1)} %convert.145, f32[2]{0:T(128)S(1)} %fusion.71, f32[2,128,640]{2,1,0:T(8,128)S(1)} %convert.144, f32[2]{0:T(128)S(1)} %fusion.72, f32[2,128,640]{2,1,0:T(8,128)S(1)} %convert.143, f32[2]{0:T(128)S(1)} %fusion.73, ...), kind=kOutput, calls=%fused_computation.40 | convolution fusion | flops 5570568 | bytes 5242938 | tf_op jit(solution)/shard_map/jl,ajtd->altd/dot_general | solution.py:114
  106.5 0.9 copy.55
  107.5 0.7 add_convert_fusion.3
  (126 shorter events, 9.1 us)
Async XLA Ops:
  0.6 5.1 %copy-start = (bf16[640,1280]{1,0:T(8,128)(2,1)S(1)}, bf16[640,1280]{1,0:T(8,128)(2,1)}, u32[]{:S(2)}) copy-start(bf16[640,1280]{1,0:T(8,128)(2,1)} %param.18) | copy-start | bytes 4915204
  4.9 5.0 %copy-start.5 = (s32[2]{0:T(128)S(1)}, s32[2]{0:T(128)}, u32[]{:S(2)}) copy-start(s32[2]{0:T(128)} %param.17) | copy-start | bytes 28
  4.9 5.0 %copy-start.6 = (s32[2]{0:T(128)S(1)}, s32[2]{0:T(128)}, u32[]{:S(2)}) copy-start(s32[2]{0:T(128)} %param.16) | copy-start | bytes 28
  4.9 5.2 %copy-start.1 = (bf16[2,2,64,640]{3,2,1,0:T(8,128)(2,1)S(1)}, bf16[2,2,64,640]{3,2,1,0:T(8,128)(2,1)}, u32[]{:S(2)}) copy-start(bf16[2,2,64,640]{3,2,1,0:T(8,128)(2,1)} %param.14) | copy-start | bytes 983044
  5.7 5.6 %copy-start.2 = (bf16[2,1280]{1,0:T(2,128)(2,1)S(1)}, bf16[2,1280]{1,0:T(2,128)(2,1)}, u32[]{:S(2)}) copy-start(bf16[2,1280]{1,0:T(2,128)(2,1)} %param.11) | copy-start | bytes 15364
  6.0 5.6 %copy-start.3 = (f32[1280]{0:T(1024)S(1)}, f32[1280]{0:T(1024)}, u32[]{:S(2)}) copy-start(f32[1280]{0:T(1024)} %param.20) | copy-start | bytes 15364
  6.0 5.6 %copy-start.4 = (f32[1280]{0:T(1024)S(1)}, f32[1280]{0:T(1024)}, u32[]{:S(2)}) copy-start(f32[1280]{0:T(1024)} %param.19) | copy-start | bytes 15364
  6.7 4.6 %all-to-all-start = ((f32[2,2,1280]{2,1,0:T(2,128)}), f32[2,2,1280]{2,1,0:T(2,128)S(1)}, u32[]{:S(2)}, u32[]{:S(2)}) async-start(f32[2,2,1280]{2,1,0:T(2,128)} %broadcast_in_dim.149), calls=%async_computation | async-start | bytes 40960 | tf_op jit(solution)/shard_map/all_to_all | solution.py:12
  17.9 64.8 %collective-permute-start.5 = (bf16[258,640]{1,0:T(8,128)(2,1)S(1)}, bf16[258,640]{1,0:T(8,128)(2,1)S(1)}, u32[]{:S(2)}, u32[]{:S(2)}) collective-permute-start(bf16[258,640]{1,0:T(8,128)(2,1)S(1)} %pad_maximum_fusion.6), channel_id=1, source_target_pairs={{250,0},{252,2},{254,4},{0,6},{2,8},{4,10},{6,12},{8,14},{10,16},{... | collective-permute-start | bytes 990728 | tf_op jit(solution)/shard_map/ppermute | solution.py:22
  24.2 63.4 %collective-permute-start.4 = (bf16[258,640]{1,0:T(8,128)(2,1)S(1)}, bf16[258,640]{1,0:T(8,128)(2,1)S(1)}, u32[]{:S(2)}, u32[]{:S(2)}) collective-permute-start(bf16[258,640]{1,0:T(8,128)(2,1)S(1)} %pad_maximum_fusion.5), channel_id=1, source_target_pairs={{252,0},{254,2},{0,4},{2,6},{4,8},{6,10},{8,12},{10,14},{12,16},{1... | collective-permute-start | bytes 990728 | tf_op jit(solution)/shard_map/ppermute | solution.py:22
  30.2 62.9 %collective-permute-start.3 = (bf16[258,640]{1,0:T(8,128)(2,1)S(1)}, bf16[258,640]{1,0:T(8,128)(2,1)S(1)}, u32[]{:S(2)}, u32[]{:S(2)}) collective-permute-start(bf16[258,640]{1,0:T(8,128)(2,1)S(1)} %pad_maximum_fusion.4), channel_id=1, source_target_pairs={{254,0},{0,2},{2,4},{4,6},{6,8},{8,10},{10,12},{12,14},{14,16},{16... | collective-permute-start | bytes 990728 | tf_op jit(solution)/shard_map/ppermute | solution.py:22
  34.3 58.8 %collective-permute-start.2 = (bf16[258,640]{1,0:T(8,128)(2,1)S(1)}, bf16[258,640]{1,0:T(8,128)(2,1)S(1)}, u32[]{:S(2)}, u32[]{:S(2)}) collective-permute-start(bf16[258,640]{1,0:T(8,128)(2,1)S(1)} %pad_maximum_fusion.3), channel_id=1, source_target_pairs={{2,0},{4,2},{6,4},{8,6},{10,8},{12,10},{14,12},{16,14},{18,16},{20... | collective-permute-start | bytes 990728 | tf_op jit(solution)/shard_map/ppermute | solution.py:22
  76.6 19.4 %collective-permute-start.1 = (bf16[258,640]{1,0:T(8,128)(2,1)S(1)}, bf16[258,640]{1,0:T(8,128)(2,1)S(1)}, u32[]{:S(2)}, u32[]{:S(2)}) collective-permute-start(bf16[258,640]{1,0:T(8,128)(2,1)S(1)} %pad_maximum_fusion.2), channel_id=1, source_target_pairs={{4,0},{6,2},{8,4},{10,6},{12,8},{14,10},{16,12},{18,14},{20,16},{2... | collective-permute-start | bytes 990728 | tf_op jit(solution)/shard_map/ppermute | solution.py:22
  82.7 20.5 %collective-permute-start = (bf16[258,640]{1,0:T(8,128)(2,1)S(1)}, bf16[258,640]{1,0:T(8,128)(2,1)S(1)}, u32[]{:S(2)}, u32[]{:S(2)}) collective-permute-start(bf16[258,640]{1,0:T(8,128)(2,1)S(1)} %pad_maximum_fusion.1), channel_id=1, source_target_pairs={{6,0},{8,2},{10,4},{12,6},{14,8},{16,10},{18,12},{20,14},{22,16},{... | collective-permute-start | bytes 990728 | tf_op jit(solution)/shard_map/ppermute | solution.py:22
where the time goes:
time: 109 us; the launch traced here: 108 us
  starting transfers between devices  66.8 us (61%)
  waiting for transfers between devices  15.8 us (14%)
  matrix products  13.4 us (12%)
  other arithmetic  5.71 us (5%)
  local copies, waits for them, and re-layouts  5.24 us (5%)
  between operations  1.3 us (1%)
    ppermute x6, starting transfers between devices, passed_along(): return lax.ppermute(block, axis, route)  63.5 us
    ppermute x6, waiting for transfers between devices, passed_along(): return lax.ppermute(block, axis, route)  15.1 us
    dot_general x6, matrix products, body(): jnp.einsum('j,ajtd->atd', picked, updated, preferred_element_type=jnp.flo...  4.96 us
    all_to_all x1, starting transfers between devices, copy_for_each(): return lax.all_to_all(copies, axis, split_axis=0, concat_axis=0, tiled=True)  3.27 us
    dot_general x1, matrix products, body(): jnp.einsum('jl,ajtd->altd', select, updated, preferred_element_type=jnp.f...  3.13 us
  transfers between devices with their start and end apart: 7, of which 4 were waited for; matrix products, arithmetic and copies ran while one was open for 6% of the time, Pallas kernels for 0%

commit v1 on v0

v1 whole, which is shorter than its diff:
```python
import functools

import jax
import jax.numpy as jnp
from jax import lax
from jax.experimental import pallas as pl
from jax.experimental.pallas import tpu as pltpu
from jax.sharding import PartitionSpec as P

HEAD_DIM = 64
REACH = 3
ROW = 4
HALVES = 2
MESH = pl.DeviceIdType.MESH
F32 = jnp.float32
BF16 = jnp.bfloat16


def spread_heads(row, rows):
    width = row.shape[-1]
    head = lax.broadcasted_iota(jnp.int32, (rows, width), 0)
    lane_head = lax.broadcasted_iota(jnp.int32, (rows, width), 1) // HEAD_DIM
    return jnp.where(head == lane_head, jnp.broadcast_to(row, (rows, width)), 0.0)


def gather_heads(product):
    rows, width = product.shape
    head = lax.broadcasted_iota(jnp.int32, (rows, width), 0)
    lane_head = lax.broadcasted_iota(jnp.int32, (rows, width), 1) // HEAD_DIM
    return jnp.sum(jnp.where(head == lane_head, product, 0.0), axis=0, keepdims=True)


def two_rows(first, second, rows):
    shape = (rows, first.shape[-1])
    at = lax.broadcasted_iota(jnp.int32, shape, 0)
    return jnp.where(at == 0, jnp.broadcast_to(first, shape), jnp.broadcast_to(second, shape))


def attend(query_row, keys, values, last):
    scores = lax.dot_general(
        spread_heads(query_row, 16).astype(BF16),
        keys,
        (((1,), (1,)), ((), ())),
        preferred_element_type=F32,
    ) * (HEAD_DIM**-0.5)
    if last is not None:
        usable = lax.broadcasted_iota(jnp.int32, scores.shape, 1) <= last
        scores = jnp.where(usable, scores, -1e30)
    weight = jnp.exp(scores - jnp.max(scores, axis=-1, keepdims=True))
    if last is not None:
        weight = jnp.where(usable, weight, 0.0)
    weight = (weight / jnp.sum(weight, axis=-1, keepdims=True)).astype(BF16)
    return gather_heads(jnp.dot(weight, values, preferred_element_type=F32))


def kernel(
    devices,
    hidden_h,
    qkv_h,
    cache_h,
    cross_h,
    len_h,
    fin_h,
    slot_h,
    wo_h,
    gain_h,
    bias_h,
    wq_h,
    moved_h,
    out_ref,
    hidden,
    qkv,
    cache,
    cross,
    lens,
    fins,
    slots,
    wo,
    gain,
    bias,
    wq,
    partial,
    arrived,
    info,
    rows_out,
    *rest,
):
    chunks = 2 * HALVES
    cands, stages = rest[:chunks], rest[chunks : 2 * chunks]
    (load_sem, own_sem, info_s, info_r, p1_s, p1_r, z_s, z_r, p3_s, p3_r, mp_s, mp_r, out_s, out_r) = rest[2 * chunks :]
    spans, positions = cache.shape[1], cache.shape[2]
    quarter = positions // ROW
    piece = quarter // HALVES
    me = lax.axis_index("batch")
    x = lax.rem(me, ROW)
    row_start = me - x
    core = lax.axis_index("mp")

    def device(dz, column):
        return {"batch": lax.rem(row_start + dz * ROW + devices, devices) + column}

    def column(dx):
        return lax.rem(x + dx + ROW, ROW)

    def remote(src, dst, send, recv, to):
        return pltpu.make_async_remote_copy(
            src_ref=src, dst_ref=dst, send_sem=send, recv_sem=recv, device_id=to, device_id_type=MESH
        )

    order = [
        (len_h, lens),
        (fin_h, fins),
        (slot_h, slots),
        (qkv_h, qkv),
        (cache_h.at[0], cache.at[0]),
        (cache_h.at[1], cache.at[1]),
        (wo_h, wo),
        (hidden_h, hidden),
        (gain_h, gain),
        (bias_h, bias),
        (wq_h, wq),
        (cross_h, cross),
    ]
    loads = [pltpu.make_async_copy(src, dst, load_sem.at[n]) for n, (src, dst) in enumerate(order)]
    for load in loads:
        load.start()

    barrier = pltpu.get_barrier_semaphore()
    peers = [(dz, dx) for dz in (0, -1, 1) for dx in range(ROW) if (dz, dx) != (0, 0)]
    for dz, dx in peers:
        pl.semaphore_signal(barrier, inc=1, device_id=device(dz, column(dx)), device_id_type=MESH)
    pl.semaphore_signal(barrier, inc=1, device_id={"mp": 1 - core}, device_id_type=MESH)

    for load in loads[:4]:
        load.wait()
    at = lax.broadcasted_iota(jnp.int32, (positions, cache.shape[3]), 0)
    for a in range(2):
        loads[4 + a].wait()
        for j in range(spans):
            older = cache[a, j].astype(F32)
            fresh = jnp.broadcast_to(qkv[1 + a, j : j + 1].astype(F32), older.shape)
            length = lens[j]
            grown = jnp.where(at < length, older, jnp.where(at == length, fresh, 0.0))
            alive = jnp.where(at < jnp.where(fins[j] == 0, positions, 0), grown, 0.0)
            cache[a, j] = alive.astype(BF16)
    for c in range(chunks):
        a, half = c // HALVES, c % HALVES
        start = pl.multiple_of(quarter * x + piece * half, piece)
        for j in range(spans):
            cands[c][spans * x + j] = cache[a, j, pl.ds(start, piece), :]
    lane = lax.broadcasted_iota(jnp.int32, (1, 128), 1)
    info[ROW + x] = jnp.where(lane == 0, slots[0], slots[1])

    pl.semaphore_wait(barrier, len(peers) + 1)

    info_copies = []
    for n, (dz, dx) in enumerate(peers):
        copy = remote(
            info.at[ROW + x], info.at[(1 - dz) * ROW + x], info_s.at[n], info_r.at[n], device(dz, column(dx))
        )
        copy.start()
        info_copies.append(copy)

    first = []
    for c in range(chunks):
        a, half = c // HALVES, c % HALVES
        for n, dx in enumerate((1, 3, 2)):
            to = column(dx)
            start = pl.multiple_of(quarter * to + piece * half, piece)
            copy = remote(
                cache.at[a, :, pl.ds(start, piece), :],
                cands[c].at[pl.ds(spans * x, spans)],
                p1_s.at[c, n],
                p1_r.at[c, n],
                device(0, to),
            )
            copy.start()
            first.append(copy)

    base_up, base_down = ROW * spans, ROW * spans + REACH * spans

    def up(c, n, b):
        return remote(
            cands[c].at[pl.ds(spans * b, spans)],
            cands[c].at[pl.ds(base_up + spans * (b - 1), spans)],
            z_s.at[c, 0, n],
            z_r.at[c, 0, b - 1],
            device(1, x),
        )

    def down(c, n, b):
        return remote(
            cands[c].at[pl.ds(spans * b, spans)],
            cands[c].at[pl.ds(base_down + spans * b, spans)],
            z_s.at[c, 1, n],
            z_r.at[c, 1, b],
            device(-1, x),
        )

    def pass_on(c, n, b):
        @pl.when(b >= 1)
        def _():
            up(c, n, b).start()

        @pl.when(b <= REACH - 1)
        def _():
            down(c, n, b).start()

    for c in range(chunks):
        pass_on(c, 0, x)

    def relay(c):
        for n, dx in enumerate((1, 3, 2)):
            first[c * 3 + n].wait_recv()
            pass_on(c, n + 1, column(-dx))

    contexts = []
    for j in range(spans):
        contexts.append(attend(qkv[0, j : j + 1].astype(F32), cache[0, j], cache[1, j], lens[j]))
    context = two_rows(contexts[0], contexts[1], 16).astype(BF16)
    loads[6].wait()
    partial[...] = jnp.dot(context, wo[...], preferred_element_type=F32)[:spans]
    swap = remote(partial, arrived, mp_s.at[0], mp_r.at[0], {"mp": 1 - core})
    swap.start()
    relay(0)
    for load in loads[7:]:
        load.wait()
    swap.wait()
    resid = hidden[...].astype(F32) + (partial[...] + arrived[...])
    centre = jnp.mean(resid, axis=-1, keepdims=True)
    spread = jnp.mean((resid - centre) ** 2, axis=-1, keepdims=True)
    normed = (resid - centre) * lax.rsqrt(spread + 1e-05) * gain[...] + bias[...]
    normed = two_rows(normed[0:1], normed[1:2], 16).astype(BF16)
    cross_query = jnp.dot(normed, wq[...], preferred_element_type=F32).astype(BF16).astype(F32)
    relay(1)
    decoded = []
    for j in range(spans):
        got = attend(cross_query[j : j + 1], cross[0, j], cross[1, j], None)
        decoded.append(jnp.where(lane[:, :1] < jnp.where(fins[j] == 0, 1, 0), got, 0.0))
    rows_out[REACH] = two_rows(decoded[0], decoded[1], spans).astype(BF16)
    out_copies = []
    for n, d in enumerate([d for d in range(-REACH, REACH + 1) if d != 0]):
        to = {"batch": lax.rem(me + d + devices, devices)}
        copy = remote(rows_out.at[REACH], rows_out.at[REACH - d], out_s.at[n], out_r.at[n], to)
        copy.start()
        out_copies.append(copy)
    relay(2)
    relay(3)

    for copy in info_copies:
        copy.wait_recv()
    table = info[...].reshape(3 * ROW, 128)
    source = lax.broadcasted_iota(jnp.int32, table.shape, 0)
    local = lax.broadcasted_iota(jnp.int32, table.shape, 1)
    source_x = source % ROW
    below, above = source < ROW, source >= 2 * ROW
    number = spans * source_x + local
    number = jnp.where(below, number + base_up - spans, jnp.where(above, number + base_down, number))
    counted = local < spans

    def look_up(slot, values, most):
        return jnp.minimum(jnp.max(jnp.where(counted & (table == slot), values, 0)), most)

    takes = [look_up(spans * row_start + n, number, cands[0].shape[0] - 1) for n in range(spans * ROW)]
    away = source - ROW - x + REACH
    mine = [
        (look_up(spans * me + n, away, 2 * REACH), look_up(spans * me + n, local, spans - 1))
        for n in range(spans)
    ]

    third = []
    owns = []
    for c in range(chunks):
        a, half = c // HALVES, c % HALVES
        for n in range(3):
            remote(cands[c].at[pl.ds(0, spans)], cands[c].at[pl.ds(base_up + spans * n, spans)], z_s.at[c, 0, n], z_r.at[c, 0, n], device(1, x)).wait_recv()
            remote(cands[c].at[pl.ds(0, spans)], cands[c].at[pl.ds(base_down + spans * n, spans)], z_s.at[c, 1, n], z_r.at[c, 1, n], device(-1, x)).wait_recv()
        for n in range(ROW):
            for l in range(spans):
                stages[c][n, l] = cands[c][takes[spans * n + l]]
        start = pl.multiple_of(quarter * x + piece * half, piece)
        where = moved_h.at[a, :, pl.ds(start, piece), :]
        for n, dx in enumerate((1, 3, 2)):
            to = column(dx)
            copy = remote(stages[c].at[to], where, p3_s.at[c, n], p3_r.at[c, n], device(0, to))
            copy.start()
            third.append(copy)
        own = pltpu.make_async_copy(stages[c].at[x], where, own_sem.at[c])
        own.start()
        owns.append(own)

    for copy in out_copies:
        copy.wait_recv()
    results = []
    for source_of, local_of in mine:
        both = rows_out[source_of].astype(F32)
        results.append(jnp.where(jnp.broadcast_to(local_of, both[:1].shape) == 0, both[0:1], both[1:2]))
    out_ref[...] = two_rows(results[0], results[1], spans).astype(BF16)

    for copy in third:
        copy.wait_recv()
    for own in owns:
        own.wait()
    for copy in info_copies + first + out_copies + third:
        copy.wait_send()
    for c in range(chunks):
        for n, dx in enumerate((0, 1, 3, 2)):
            b = column(-dx)

            @pl.when(b >= 1)
            def _():
                up(c, n, b).wait_send()

            @pl.when(b <= REACH - 1)
            def _():
                down(c, n, b).wait_send()


def body(
    hidden,
    token_qkv,
    self_cache,
    cross_kv,
    cache_len,
    finished,
    new_slot,
    out_proj,
    ln_gain,
    ln_bias,
    query_proj,
):
    spans, full_width = hidden.shape
    _, _, slots, width = self_cache.shape
    chunks = 2 * HALVES
    piece = slots // ROW // HALVES
    dma, vmem, smem = pltpu.SemaphoreType.DMA, pltpu.VMEM, pltpu.SMEM
    gain, bias = ln_gain.reshape(1, -1), ln_bias.reshape(1, -1)
    inputs = (hidden, token_qkv, self_cache, cross_kv, cache_len, finished, new_slot, out_proj, gain, bias, query_proj)
    peers = 3 * ROW - 1
    candidates = spans * (ROW + 2 * REACH)
    scratch = [
        vmem(hidden.shape, BF16),
        vmem(token_qkv.shape, BF16),
        vmem(self_cache.shape, BF16),
        vmem(cross_kv.shape, BF16),
        smem(cache_len.shape, jnp.int32),
        smem(finished.shape, jnp.int32),
        smem(new_slot.shape, jnp.int32),
        vmem(out_proj.shape, BF16),
        vmem(gain.shape, F32),
        vmem(bias.shape, F32),
        vmem(query_proj.shape, BF16),
        vmem((spans, full_width), F32),
        vmem((spans, full_width), F32),
        vmem((3 * ROW, 1, 128), jnp.int32),
        vmem((2 * REACH + 1, spans, width), BF16),
        *[vmem((candidates, piece, width), BF16) for _ in range(chunks)],
        *[vmem((ROW, spans, piece, width), BF16) for _ in range(chunks)],
        dma((len(inputs) + 1,)),
        dma((chunks,)),
        dma((peers,)),
        dma((peers,)),
        dma((chunks, 3)),
        dma((chunks, 3)),
        dma((chunks, 2, ROW)),
        dma((chunks, 2, 3)),
        dma((chunks, 3)),
        dma((chunks, 3)),
        dma((1,)),
        dma((1,)),
        dma((2 * REACH,)),
        dma((2 * REACH,)),
    ]
    return pl.pallas_call(
        functools.partial(kernel, lax.axis_size("batch")),
        out_shape=(
            jax.ShapeDtypeStruct(self_cache.shape, BF16),
            jax.ShapeDtypeStruct((spans, width), BF16),
        ),
        in_specs=[pl.BlockSpec(memory_space=pl.ANY)] * len(inputs),
        out_specs=(pl.BlockSpec(memory_space=pl.ANY), pl.BlockSpec(memory_space=vmem)),
        scratch_shapes=scratch,
        compiler_params=pltpu.CompilerParams(collective_id=0, has_side_effects=True),
    )(*inputs)


def solution(mesh):
    placed = (
        P(("groups", "batch"), None),
        P(None, ("groups", "batch"), "mp"),
        P(None, ("groups", "batch"), None, "mp"),
        P(None, ("groups", "batch"), None, "mp"),
        P(("groups", "batch")),
        P(("groups", "batch")),
        P(("groups", "batch")),
        P("mp", None),
        P(),
        P(),
        P(None, "mp"),
    )
    return jax.shard_map(
        body,
        mesh=mesh,
        in_specs=placed,
        out_specs=(P(None, ("groups", "batch"), None, "mp"), P(("groups", "batch"), "mp")),
        check_vma=False,
    )
```

time: 109 us -> 74.3 us (0.68)
  Pallas kernels: 0 us -> 67.6 us
  starting transfers between devices: 66.8 us -> 0 us
  waiting for transfers between devices: 15.8 us -> 0 us
  matrix products: 13.4 us -> 0 us
  other arithmetic: 5.71 us -> 0 us
    pallas_call x0 -> x1, Pallas kernels: none -> 67.6 us  [body(): pl.pallas_call(functools.partial(kernel, lax.axis_size('batch')), out_sha...]
    ppermute x6 -> x0, starting transfers between devices: 63.5 us -> none  [passed_along(): return lax.ppermute(block, axis, route)]
    ppermute x6 -> x0, waiting for transfers between devices: 15.1 us -> none  [passed_along(): return lax.ppermute(block, axis, route)]
    dot_general x26 -> x0, matrix products: 13.4 us -> none  [the longest x6 4.96 us: body(): jnp.einsum('j,ajtd->atd', picked, updated, preferred_element_type=jnp.flo...]
    all_to_all x1 -> x0, starting transfers between devices: 3.27 us -> none  [copy_for_each(): return lax.all_to_all(copies, axis, split_axis=0, concat_axis=0, tiled=True)]
    reshape x3 -> x2, local copies, waits for them, and re-layouts: 0.28 us -> 2.59 us  [body(): gain, bias = (ln_gain.reshape(1, -1), ln_bias.reshape(1, -1))]
    unnamed x17 -> x2, local copies, waits for them, and re-layouts: 1.39 us -> 3.22 us
    slice x10 -> x0, local copies, waits for them, and re-layouts: 1.8 us -> none  [the longest x2 1.37 us: body(): self_cache[0]]
  transfers between devices with their start and end apart: 7 -> 0, of which waited for: 4 -> 0; matrix products, arithmetic and copies ran while one was open for 6% -> 0% of each run, Pallas kernels for 0% -> 0%
where the time goes in v1:
time: 74.3 us; the launch traced here: 74 us
  Pallas kernels  67.6 us (91%)
  local copies, waits for them, and re-layouts  5.81 us (8%)
    pallas_call x1, Pallas kernels, body(): pl.pallas_call(functools.partial(kernel, lax.axis_size('batch')), out_sha...  67.6 us
    unnamed x2, local copies, waits for them, and re-layouts  3.22 us
    reshape x2, local copies, waits for them, and re-layouts, body(): gain, bias = (ln_gain.reshape(1, -1), ln_bias.reshape(1, -1))  2.59 us

profile of v1, /device:TPU:40, one launch (start us, length us, event | category | flops | bytes accessed | tf_op | source)
XLA Modules:
  0.0 74.0 jit_solution(11142170425757187184)
XLA Ops:
  0.6 1.3 %reshape.10.gain_h = f32[1,1280]{1,0:T(1,128)} reshape(f32[1280]{0:T(1024)} %param.19) | data formatting | bytes 10240 | tf_op jit(solution)/shard_map/reshape | solution.py:337
  1.9 1.3 %reshape.11.bias_h = f32[1,1280]{1,0:T(1,128)} reshape(f32[1280]{0:T(1024)} %param.20) | data formatting | bytes 10240 | tf_op jit(solution)/shard_map/reshape | solution.py:337
  3.2 67.6 %shard_map.122 = (bf16[2,2,128,640]{3,2,1,0:T(8,128)(2,1)}, bf16[2,640]{1,0:T(2,128)(2,1)}) custom-call(bf16[2,1280]{1,0:T(2,128)(2,1)} %hidden_h.1, bf16[3,2,640]{2,1,0:T(2,128)(2,1)} %qkv_h.1, bf16[2,2,128,640]{3,2,1,0:T(8,128)(2,1)} %cache_h.1, bf16[2,2,64,640]{3,2,1,0:T(8,128)(2,1)} %cross_h.1, s32[2]{0:T(128)} %len_h.1, s32[2]{0:T(128)} %fin_h.1, ...), custom_call_target="tpu_custom_call" | custom-call | tf_op jit(solution)/shard_map/pallas_call | solution.py:374
  70.8 2.0 %copy.15 = bf16[2,2,128,640]{3,2,1,0:T(8,128)(2,1)} copy(bf16[2,2,128,640]{3,2,1,0:T(8,128)(2,1)} %get-tuple-element.4) | data formatting | bytes 1310720
  72.8 1.2 %copy.16 = bf16[2,640]{1,0:T(2,128)(2,1)} copy(bf16[2,640]{1,0:T(2,128)(2,1)} %get-tuple-element.5) | data formatting | bytes 5120
